TPU v7x, 32 devices: a whole 2x2x4 slice. The times are simulated.
32 devices in a mesh: seq: 8 (over z, y), grp: 4 (over x, core).
Axes of the slice: x: 2, y: 2, z: 4, core: 2. Of those that a mesh axis runs over, the one named last changes fastest.
Arguments:
- query_nope: bfloat16 [4, 2, 128, 128], P(None, None, 'seq'), may hold values from -12.859821 to 12.859821
- query_rope: bfloat16 [4, 2, 128, 64], P(None, None, 'seq'), may hold values from -150 to 150
- latent_cache: bfloat16 [4, 8192, 576], P(None, ('seq', 'grp')), may hold values from -5 to 5
- lengths: int32 [4], replicated, may hold values from 4096 to 8192
- key_weight: bfloat16 [128, 128, 512], P('seq'), may hold values from -0.5 to 0.5
- value_weight: bfloat16 [128, 512, 128], P('seq'), may hold values from -0.25 to 0.25
- output_weight: bfloat16 [16384, 7168], P('seq', 'grp'), may hold values from -0.0625 to 0.0625
Outputs:
- mixed: bfloat16 [4, 2, 7168], P(None, None, ('grp', 'seq'))
All inputs are finite; a program needn't handle non-finite values.
Results may differ from a plain program's by a relative error of at most 0.0095.
Values may be sent and summed in bfloat16 or wider, within the bound.
No kernel may reach another device: no remote copies, remote signals or barrier semaphores. Data moves between devices by JAX's collectives and lax.ppermute only.
A program may use at most 64 MiB of HBM per device.

v0:
```python
import jax
import jax.numpy as jnp
from jax import lax
from jax.sharding import PartitionSpec as P

NEGATIVE = -1e30


def joined(part, axis, combine):
    gathered = jax.tree.map(lambda a: lax.all_gather(a, axis), part)

    def take(source):
        return jax.tree.map(lambda a: lax.dynamic_index_in_dim(a, source, 0, False), gathered)

    return lax.fori_loop(
        1, lax.axis_size(axis), lambda source, state: combine(state, take(source)), take(0)
    )


def shard_partial(queries, cache_block, limits, offset, factor, latent_width):
    raw_score = (
        jnp.einsum("bqhd,bpd->bqhp", queries, cache_block, preferred_element_type=jnp.float32)
        * factor
    )
    places = offset + lax.broadcasted_iota(jnp.int32, (1, 1, cache_block.shape[1]), 2)
    visible = places < limits[:, :, None]
    scores = jnp.where(visible[:, :, None, :], raw_score, NEGATIVE)
    maxima = jnp.max(scores, axis=-1)
    powers = jnp.exp(scores - maxima[..., None])
    totals = jnp.sum(powers, axis=-1)
    weights = powers.astype(jnp.bfloat16)
    summed = jnp.einsum(
        "bqhp,bpd->bqhd",
        weights,
        cache_block[:, :, :latent_width],
        preferred_element_type=jnp.float32,
    )
    return (maxima, totals, (summed / totals[..., None]).astype(jnp.bfloat16))


def merge_sources(partials, maxima, totals):
    highest = jnp.max(maxima, axis=0)
    shares = totals * jnp.exp(maxima - highest[None])
    summed = jnp.sum(shares, axis=0)
    numerator = jnp.sum(shares[..., None] * partials.astype(jnp.float32), axis=0)
    return (highest, summed, numerator / summed[..., None])


def merge_tuple(received):
    return merge_sources(received[0], received[1], received[2])


def join_pairs(earlier, later):
    highest = jnp.maximum(earlier[0], later[0])
    left_share = earlier[1] * jnp.exp(earlier[0] - highest)
    right_share = later[1] * jnp.exp(later[0] - highest)
    summed = left_share + right_share
    blended = (left_share[..., None] * earlier[2] + right_share[..., None] * later[2]) / summed[
        ..., None
    ]
    return (highest, summed, blended)


def absorb(query_nope, query_rope, key_weight):
    absorbed = jnp.einsum(
        "bqhn,hnd->bqhd", query_nope, key_weight, preferred_element_type=jnp.float32
    )
    return jnp.concatenate([absorbed.astype(jnp.bfloat16), query_rope], axis=-1)


def up_project(latent_out, value_weight):
    values = jnp.einsum(
        "bqhd,hde->bqhe", latent_out, value_weight, preferred_element_type=jnp.float32
    ).astype(jnp.bfloat16)
    return values.reshape(values.shape[0], values.shape[1], values.shape[2] * values.shape[3])


def shards(query_nope, query_rope, latent_cache, lengths, key_weight, value_weight, output_weight):
    latent_width = key_weight.shape[2]
    factor = float(query_nope.shape[3] + query_rope.shape[3]) ** (-0.5)
    positions = latent_cache.shape[1]
    drafts = query_nope.shape[1]
    offset = (lax.axis_index("seq") * lax.axis_size("grp") + lax.axis_index("grp")) * positions
    limits = lengths[:, None] - drafts + 1 + lax.broadcasted_iota(jnp.int32, (1, drafts), 1)
    own_queries = absorb(query_nope, query_rope, key_weight)
    maxima, totals, partials = shard_partial(
        lax.all_gather(own_queries, "seq", axis=2, tiled=True),
        latent_cache,
        limits,
        offset,
        factor,
        latent_width,
    )
    partials, maxima, totals = (partials, maxima, totals)
    sources = (partials[None], maxima[None], totals[None])
    gathered = merge_tuple(
        (
            lax.all_to_all(
                sources[0].astype(jnp.float32), "seq", split_axis=3, concat_axis=0, tiled=True
            ).astype(jnp.bfloat16),
            lax.all_to_all(sources[1], "seq", split_axis=3, concat_axis=0, tiled=True),
            lax.all_to_all(sources[2], "seq", split_axis=3, concat_axis=0, tiled=True),
        )
    )
    highest, summed, blended = joined((gathered[0], gathered[1], gathered[2]), "grp", join_pairs)
    values = up_project(blended.astype(jnp.bfloat16), value_weight)
    head_terms = jnp.dot(values, output_weight, preferred_element_type=jnp.float32)
    reduced = lax.psum_scatter(head_terms, "seq", scatter_dimension=2, tiled=True)
    return reduced.astype(jnp.bfloat16)


def solution(mesh):
    in_specs = (
        P(None, None, "seq", None),
        P(None, None, "seq", None),
        P(None, ("seq", "grp"), None),
        P(),
        P("seq", None, None),
        P("seq", None, None),
        P("seq", "grp"),
    )
    out_specs = P(None, None, ("grp", "seq"))
    return jax.shard_map(shards, mesh=mesh, in_specs=in_specs, out_specs=out_specs, check_vma=False)
```

profile of v0, /device:TPU:0, one launch (start us, length us, event | category | flops | bytes accessed | tf_op | source)
XLA Modules:
  0.0 212.3 jit_solution(17703678175560071938)
XLA Ops:
  6.5 0.9 copy.29
  7.5 0.7 copy-done
  8.1 1.1 fusion.18
  9.3 0.8 pad_maximum_fusion
  10.2 44.5 %all-gather.5.cloned.1.call-done = bf16[4,2,128,576]{3,0,1,2:T(4,128)(2,1)} async-done(((bf16[4,2,16,576]{3,0,1,2:T(4,128)(2,1)}), bf16[4,2,128,576]{3,0,1,2:T(4,128)(2,1)}) %all-gather.5.cloned.1.call-update) | async-done | bytes 1179664 | tf_op jit(solution)/shard_map/all_gather | solution.py:87
  54.7 2.4 %fusion.42 = (f32[4,2,128]{2,1,0:T(2,128)S(1)}, f32[4,2,128,256]{3,2,1,0:T(8,128)S(1)}) fusion(bf16[4,256,576]{1,2,0:T(8,128)(2,1)} %param.11, bf16[4,2,128,576]{3,0,1,2:T(4,128)(2,1)} %all-gather.5.cloned.1.call-done, pred[4,2,256]{2,1,0:T(4,128)(4,1)S(1)} %broadcast_compare_fusion), kind=kOutput, calls=%fused_computation.50 | convolution fusion | flops 302775296 | bytes 3414016 | tf_op jit(solution)/shard_map/bqhd,bpd->bqhp/dot_general | solution.py:22
  57.1 0.4 fusion.30
  57.5 0.2 copy.34
  57.7 0.8 reshape.85
  58.5 3.4 %all-to-all-start.1 = ((f32[8,1,128]{2,1,0:T(1,128)}), f32[8,1,128]{2,1,0:T(1,128)S(1)}, u32[]{:S(2)}, u32[]{:S(2)}) async-start(f32[8,1,128]{2,1,0:T(1,128)} %reshape.85), calls=%async_computation.1 | async-start | bytes 8192 | tf_op jit(solution)/shard_map/all_to_all | solution.py:102
  61.9 0.2 copy.31
  62.1 0.8 reshape.83
  62.9 5.5 %all-to-all-done.1 = f32[8,1,128]{2,1,0:T(1,128)S(1)} async-done(((f32[8,1,128]{2,1,0:T(1,128)}), f32[8,1,128]{2,1,0:T(1,128)S(1)}, u32[]{:S(2)}, u32[]{:S(2)}) %all-to-all-start.1) | async-done | bytes 4128 | tf_op jit(solution)/shard_map/all_to_all | solution.py:102
  68.4 3.3 %all-to-all-start = ((f32[8,1,128]{2,1,0:T(1,128)}), f32[8,1,128]{2,1,0:T(1,128)S(1)}, u32[]{:S(2)}, u32[]{:S(2)}) async-start(f32[8,1,128]{2,1,0:T(1,128)} %reshape.83), calls=%async_computation | async-start | bytes 8192 | tf_op jit(solution)/shard_map/all_to_all | solution.py:101
  71.7 1.7 fusion.11
  73.5 2.1 copy.38
  75.6 2.5 %all-to-all-done = f32[8,1,128]{2,1,0:T(1,128)S(1)} async-done(((f32[8,1,128]{2,1,0:T(1,128)}), f32[8,1,128]{2,1,0:T(1,128)S(1)}, u32[]{:S(2)}, u32[]{:S(2)}) %all-to-all-start) | async-done | bytes 4128 | tf_op jit(solution)/shard_map/all_to_all | solution.py:101
  78.1 3.6 %all-to-all-start.2 = ((bf16[1,4,2,128,512]{4,2,1,0,3:T(2,128)(2,1)}), bf16[1,4,2,128,512]{4,2,1,0,3:T(2,128)(2,1)S(1)}, u32[]{:S(2)}, u32[]{:S(2)}) async-start(bf16[1,4,2,128,512]{4,2,1,0,3:T(2,128)(2,1)} %copy.38), calls=%async_computation.2 | async-start | bytes 2097152 | tf_op jit(solution)/shard_map/all_to_all | solution.py:98
  81.7 0.5 broadcast.51
  82.2 0.7 reduce.2
  82.9 0.2 reshape.86
  83.1 1.6 copy.35
  84.7 0.7 reduce.1
  85.4 0.2 reshape.84
  85.6 0.9 copy.32
  86.6 1.8 fusion.40
  88.4 16.5 %all-to-all-done.2 = bf16[1,4,2,128,512]{4,2,1,0,3:T(2,128)(2,1)S(1)} async-done(((bf16[1,4,2,128,512]{4,2,1,0,3:T(2,128)(2,1)}), bf16[1,4,2,128,512]{4,2,1,0,3:T(2,128)(2,1)S(1)}, u32[]{:S(2)}, u32[]{:S(2)}) %all-to-all-start.2) | async-done | bytes 1048608 | tf_op jit(solution)/shard_map/all_to_all | solution.py:98
  104.9 2.3 %fusion.7 = f32[4,2,16,512]{3,1,0,2:T(2,128)S(1)} fusion(bf16[1,4,2,8,16,512]{5,2,1,4,3,0:T(2,128)(2,1)S(1)} %bitcast.108, f32[8,4,2,16]{2,1,3,0:T(4,128)} %get-tuple-element.201), kind=kLoop, calls=%fused_computation.13 | loop fusion | flops 1507328 | bytes 1314816 | tf_op jit(solution)/shard_map/reduce_sum | solution.py:45
  107.2 0.2 bitcast_divide_fusion
  107.3 0.9 copy.39
  108.3 0.1 copy.33
  108.4 0.1 copy.36
  108.5 5.2 %all-gather.1 = f32[16,2,16]{2,1,0:T(2,128)S(1)} all-gather(f32[4,2,16]{2,1,0:T(2,128)S(1)} %copy.36), channel_id=3, replica_groups=mesh['seq'=8,'grp'=4] {'grp'}, dimensions={0}, use_global_device_ids=true | all-gather | bytes 2560 | tf_op jit(solution)/shard_map/all_gather | solution.py:10
  113.7 5.2 %all-gather = f32[16,2,16]{2,1,0:T(2,128)S(1)} all-gather(f32[4,2,16]{2,1,0:T(2,128)S(1)} %copy.33), channel_id=2, replica_groups=mesh['seq'=8,'grp'=4] {'grp'}, dimensions={0}, use_global_device_ids=true | all-gather | bytes 2560 | tf_op jit(solution)/shard_map/all_gather | solution.py:10
  118.9 5.1 %all-gather.7.cloned.1.call-done = f32[4,4,2,16,512]{4,3,2,1,0:T(8,128)} async-done(((f32[1,4,2,16,512]{4,3,2,1,0:T(8,128)}), f32[4,4,2,16,512]{4,3,2,1,0:T(8,128)}) %all-gather.7.cloned.1.call-update) | async-done | bytes 1048592 | tf_op jit(solution)/shard_map/all_gather | solution.py:10
  124.0 1.0 slice_bitcast_fusion
  124.9 3.5 %while.19 = (s32[]{:T(128)}, f32[4,2,16]{2,1,0:T(2,128)S(1)}, f32[4,2,16]{2,1,0:T(2,128)S(1)}, f32[4,2,16,512]{3,2,1,0:T(8,128)S(1)}, f32[4,4,2,16]{3,2,1,0:T(2,...) while((s32[]{:T(128)}, f32[4,2,16]{2,1,0:T(2,128)S(1)}, ...), condition=%wide.region_6.7_spmd, body=%wide.region_5.6_spmd.sunk | while | flops 262917 | bytes 792207 | solution.py:15
  125.0 1.1 fusion.46
  126.2 1.1 fusion.46
  127.3 1.1 fusion.46
  128.4 2.0 fusion.24
  130.5 4.2 %fusion.3 = f32[4,2,1792]{2,0,1:T(4,128)S(1)} fusion(bf16[2048,1792]{1,0:T(8,128)(2,1)} %param.15, bf16[16,2,1,4,128]{4,3,2,1,0:T(4,128)(2,1)S(1)} %fusion.24), kind=kOutput, calls=%fused_computation.8 | convolution fusion | flops 58720256 | bytes 7430144 | tf_op jit(solution)/shard_map/dot_general | solution.py:107
  134.7 2.3 %copy.49 = f32[4,2,1792]{0,1,2:T(2,128)} copy(f32[4,2,1792]{2,0,1:T(4,128)S(1)} %fusion.3) | data formatting | bytes 114688
  137.0 3.1 %reshape.81 = f32[1792,8]{1,0:T(8,128)} reshape(f32[1792,2,4]{2,1,0:T(2,128)} %bitcast.107) | data formatting | bytes 114688
  140.1 63.9 %reduce-scatter.4.cloned.1.call-done = f32[224,8]{1,0:T(8,128)} async-done(((f32[1792,8]{1,0:T(8,128)}), f32[224,8]{1,0:T(8,128)}) %reduce-scatter.4.cloned.1.call-update) | async-done | bytes 7184
  204.0 1.0 reshape.82
  205.0 0.1 copy.50
  205.1 0.6 copy.43
  (20 shorter events, 0.5 us)
Async XLA Ops:
  6.5 1.6 copy-start
  6.5 3.5 %copy-start.1 = (s32[4]{0:T(128)S(1)}, s32[4]{0:T(128)}, u32[]{:S(2)}) copy-start(s32[4]{0:T(128)} %param.12) | copy-start | bytes 52
  6.5 48.2 %all-gather.5.cloned.1.call-start = ((), (), s32[]{:S(2)}) async-start(), calls=%async_computation.4 | async-start | bytes 1474560 | tf_op jit(solution)/shard_map/all_gather | solution.py:87
  58.5 9.9 %all-to-all-start.1 = ((f32[8,1,128]{2,1,0:T(1,128)}), f32[8,1,128]{2,1,0:T(1,128)S(1)}, u32[]{:S(2)}, u32[]{:S(2)}) async-start(f32[8,1,128]{2,1,0:T(1,128)} %reshape.85), calls=%async_computation.1 | async-start | bytes 8192 | tf_op jit(solution)/shard_map/all_to_all | solution.py:102
  68.4 9.7 %all-to-all-start = ((f32[8,1,128]{2,1,0:T(1,128)}), f32[8,1,128]{2,1,0:T(1,128)S(1)}, u32[]{:S(2)}, u32[]{:S(2)}) async-start(f32[8,1,128]{2,1,0:T(1,128)} %reshape.83), calls=%async_computation | async-start | bytes 8192 | tf_op jit(solution)/shard_map/all_to_all | solution.py:101
  78.1 26.8 %all-to-all-start.2 = ((bf16[1,4,2,128,512]{4,2,1,0,3:T(2,128)(2,1)}), bf16[1,4,2,128,512]{4,2,1,0,3:T(2,128)(2,1)S(1)}, u32[]{:S(2)}, u32[]{:S(2)}) async-start(bf16[1,4,2,128,512]{4,2,1,0,3:T(2,128)(2,1)} %copy.38), calls=%async_computation.2 | async-start | bytes 2097152 | tf_op jit(solution)/shard_map/all_to_all | solution.py:98
  81.6 42.3 %all-gather.7.cloned.1.call-start = ((), (), s32[]{:S(2)}) async-start(), calls=%async_computation.5 | async-start | bytes 1310720 | tf_op jit(solution)/shard_map/all_gather | solution.py:10
  108.2 95.8 %reduce-scatter.4.cloned.1.call-start = ((), (), s32[]{:S(2)}) async-start(), calls=%async_computation.6 | async-start | bytes 1032192
Sparse Core Ops, SparseCore 0:
  10.2 44.5 all-gather.4
  108.4 15.5 all-gather.6
  140.3 63.6 reduce-scatter.3
where the time goes:
time: 213 us; the launch traced here: 212 us
  waiting for transfers between devices  138 us (65%)
  local copies, waits for them, and re-layouts  18.2 us (9%)
  between operations  13.3 us (6%)
  matrix products  11.5 us (5%)
  starting transfers between devices  10.4 us (5%)
  blocking collectives  10.4 us (5%)
  other arithmetic  10.3 us (5%)
    unnamed x4, waiting for transfers between devices  63.9 us
    all_gather x1, waiting for transfers between devices, shards(): lax.all_gather(own_queries, 'seq', axis=2, tiled=True)  44.5 us
    all_to_all x1, waiting for transfers between devices, shards(): lax.all_to_all(sources[0].astype(jnp.float32), 'seq', split_axis=3, conca...  16.5 us
    all_gather x2, blocking collectives, joined(): gathered = jax.tree.map(lambda a: lax.all_gather(a, axis), part)  10.4 us
    unnamed x13, local copies, waits for them, and re-layouts  10.2 us
    all_to_all x1, waiting for transfers between devices, shards(): lax.all_to_all(sources[2], 'seq', split_axis=3, concat_axis=0, tiled=True)  5.53 us
    all_gather x1, waiting for transfers between devices, joined(): gathered = jax.tree.map(lambda a: lax.all_gather(a, axis), part)  5.1 us
  transfers between devices with their start and end apart: 6, of which 6 were waited for; matrix products, arithmetic and copies ran while one was open for 6% of the time, Pallas kernels for 0%

commit v1 on v0

--- a/solution.py
+++ b/solution.py
@@ -2,8 +2,22 @@
 import jax.numpy as jnp
 from jax import lax
 from jax.sharding import PartitionSpec as P
+from jax.lax import all_to_all, psum
 
 NEGATIVE = -1e30
+
+
+def review_thing(sheet, which_axis):
+    top = jnp.concatenate(
+        all_to_all(
+            jnp.stack(jnp.split(sheet, psum(1, axis_name=which_axis), axis=3)),
+            axis_name=which_axis,
+            split_axis=0,
+            concat_axis=0,
+        ),
+        axis=0,
+    )
+    return top
 
 
 def joined(part, axis, combine):
@@ -95,9 +109,7 @@
     sources = (partials[None], maxima[None], totals[None])
     gathered = merge_tuple(
         (
-            lax.all_to_all(
-                sources[0].astype(jnp.float32), "seq", split_axis=3, concat_axis=0, tiled=True
-            ).astype(jnp.bfloat16),
+            review_thing(sources[0].astype(jnp.float32), which_axis="seq").astype(jnp.bfloat16),
             lax.all_to_all(sources[1], "seq", split_axis=3, concat_axis=0, tiled=True),
             lax.all_to_all(sources[2], "seq", split_axis=3, concat_axis=0, tiled=True),
         )

time: 213 us -> 212 us (level)
  waiting for transfers between devices: 138 us -> 143 us
  other arithmetic: 10.3 us -> 7.18 us
    all_to_all x1, waiting for transfers between devices: 16.5 us -> 19.8 us  [review_thing(): all_to_all(jnp.stack(jnp.split(sheet, psum(1, axis_name=which_axis), axis...]
    unnamed x13 -> x26, local copies, waits for them, and re-layouts: 10.2 us -> 13 us
  transfers between devices with their start and end apart: 6 -> 6, of which waited for: 6 -> 6; matrix products, arithmetic and copies ran while one was open for 6% -> 3% of each run, Pallas kernels for 0% -> 0%
where the time goes in v1:
time: 212 us; the launch traced here: 211 us
  waiting for transfers between devices  143 us (67%)
  local copies, waits for them, and re-layouts  16.7 us (8%)
  between operations  13.3 us (6%)
  starting transfers between devices  10.4 us (5%)
  matrix products  10.4 us (5%)
  blocking collectives  10.4 us (5%)
  other arithmetic  7.18 us (3%)
    unnamed x4, waiting for transfers between devices  63.9 us
    all_gather x1, waiting for transfers between devices, shards(): lax.all_gather(own_queries, 'seq', axis=2, tiled=True)  44.5 us
    all_to_all x1, waiting for transfers between devices, review_thing(): all_to_all(jnp.stack(jnp.split(sheet, psum(1, axis_name=which_axis), axis...  19.8 us
    unnamed x26, local copies, waits for them, and re-layouts  13 us
    all_gather x2, blocking collectives, joined(): gathered = jax.tree.map(lambda a: lax.all_gather(a, axis), part)  10.4 us
    all_gather x1, waiting for transfers between devices, joined(): gathered = jax.tree.map(lambda a: lax.all_gather(a, axis), part)  5.3 us
    all_to_all x1, waiting for transfers between devices, shards(): lax.all_to_all(sources[2], 'seq', split_axis=3, concat_axis=0, tiled=True)  4.61 us
    all_to_all x1, waiting for transfers between devices, shards(): lax.all_to_all(sources[1], 'seq', split_axis=3, concat_axis=0, tiled=True)  4.44 us
  transfers between devices with their start and end apart: 6, of which 6 were waited for; matrix products, arithmetic and copies ran while one was open for 3% of the time, Pallas kernels for 0%

profile of v1, /device:TPU:0, one launch (start us, length us, event | category | flops | bytes accessed | tf_op | source)
XLA Modules:
  0.0 211.0 jit_solution(3330645228296328237)
XLA Ops:
  6.5 0.9 copy.32
  7.5 0.7 copy-done
  8.1 1.1 fusion.18
  9.3 0.8 pad_maximum_fusion
  10.2 0.1 broadcast_compare_fusion
  10.3 44.5 %all-gather.5.cloned.1.call-done = bf16[4,2,128,576]{3,0,1,2:T(4,128)(2,1)} async-done(((bf16[4,2,16,576]{3,0,1,2:T(4,128)(2,1)}), bf16[4,2,128,576]{3,0,1,2:T(4,128)(2,1)}) %all-gather.5.cloned.1.call-update) | async-done | bytes 1179664 | tf_op jit(solution)/shard_map/all_gather | solution.py:101
  54.8 2.5 %fusion.50 = (f32[4,2,128]{2,1,0:T(2,128)S(1)}, f32[4,2,128,256]{3,2,1,0:T(8,128)S(1)}) fusion(bf16[4,256,576]{1,2,0:T(8,128)(2,1)} %param.11, bf16[4,2,128,576]{3,0,1,2:T(4,128)(2,1)} %all-gather.5.cloned.1.call-done, pred[4,2,256]{2,1,0:T(4,128)(4,1)S(1)} %broadcast_compare_fusion), kind=kOutput, calls=%fused_computation.66 | convolution fusion | flops 302775296 | bytes 3414016 | tf_op jit(solution)/shard_map/bqhd,bpd->bqhp/dot_general | solution.py:36
  57.2 0.4 fusion.30
  57.6 0.5 fusion.11
  58.3 0.9 copy-done.2
  59.2 0.2 copy.36
  59.3 0.8 reshape.82
  60.1 3.4 %all-to-all-start.1 = ((f32[8,1,128]{2,1,0:T(1,128)}), f32[8,1,128]{2,1,0:T(1,128)S(1)}, u32[]{:S(2)}, u32[]{:S(2)}) async-start(f32[8,1,128]{2,1,0:T(1,128)} %reshape.82), calls=%async_computation.1 | async-start | bytes 8192 | tf_op jit(solution)/shard_map/all_to_all | solution.py:114
  63.5 0.9 fusion.34
  64.5 0.2 copy.34
  64.6 0.8 reshape.80
  65.4 4.6 %all-to-all-done.1 = f32[8,1,128]{2,1,0:T(1,128)S(1)} async-done(((f32[8,1,128]{2,1,0:T(1,128)}), f32[8,1,128]{2,1,0:T(1,128)S(1)}, u32[]{:S(2)}, u32[]{:S(2)}) %all-to-all-start.1) | async-done | bytes 4128 | tf_op jit(solution)/shard_map/all_to_all | solution.py:114
  70.0 3.3 %all-to-all-start = ((f32[8,1,128]{2,1,0:T(1,128)}), f32[8,1,128]{2,1,0:T(1,128)S(1)}, u32[]{:S(2)}, u32[]{:S(2)}) async-start(f32[8,1,128]{2,1,0:T(1,128)} %reshape.80), calls=%async_computation | async-start | bytes 8192 | tf_op jit(solution)/shard_map/all_to_all | solution.py:113
  73.3 0.9 fusion.33
  74.3 1.0 copy-done.1
  75.3 4.4 %all-to-all-done = f32[8,1,128]{2,1,0:T(1,128)S(1)} async-done(((f32[8,1,128]{2,1,0:T(1,128)}), f32[8,1,128]{2,1,0:T(1,128)S(1)}, u32[]{:S(2)}, u32[]{:S(2)}) %all-to-all-start) | async-done | bytes 4128 | tf_op jit(solution)/shard_map/all_to_all | solution.py:113
  79.7 3.6 %all-to-all-start.2 = ((bf16[8,1,4,2,16,512]{5,4,3,2,1,0:T(8,128)(2,1)}), bf16[8,1,4,2,16,512]{5,4,3,2,1,0:T(8,128)(2,1)S(1)}, u32[]{:S(2)}, u32[]{:S(2)}) async-start(bf16[8,1,4,2,16,512]{5,4,3,2,1,0:T(8,128)(2,1)} %copy-done.1), calls=%async_computation.2 | async-start | bytes 2097152 | tf_op jit(solution)/shard_map/all_to_all | solution.py:12
  83.3 0.5 broadcast.51
  83.8 0.7 reduce.2
  84.5 0.2 reshape.83
  84.7 0.2 copy.49
  84.9 0.7 reduce.1
  85.6 0.2 reshape.81
  85.8 0.2 copy.48
  86.1 19.8 %all-to-all-done.2 = bf16[8,1,4,2,16,512]{5,4,3,2,1,0:T(8,128)(2,1)S(1)} async-done(((bf16[8,1,4,2,16,512]{5,4,3,2,1,0:T(8,128)(2,1)}), bf16[8,1,4,2,16,512]{5,4,3,2,1,0:T(8,128)(2,1)S(1)}, u32[]{:S(2)}, u32[]{:S(2)}) %all-to-all-start.2) | async-done | bytes 1048608 | tf_op jit(solution)/shard_map/all_to_all | solution.py:12
  105.9 0.3 fusion.7
  106.2 0.8 bitcast_divide_fusion
  107.0 5.2 %all-gather.1 = f32[16,2,16]{2,1,0:T(2,128)S(1)} all-gather(f32[4,2,16]{2,1,0:T(2,128)S(1)} %get-tuple-element.200), channel_id=3, replica_groups=mesh['seq'=8,'grp'=4] {'grp'}, dimensions={0}, use_global_device_ids=true | all-gather | bytes 2560 | tf_op jit(solution)/shard_map/all_gather | solution.py:24
  112.2 5.2 %all-gather = f32[16,2,16]{2,1,0:T(2,128)S(1)} all-gather(f32[4,2,16]{2,1,0:T(2,128)S(1)} %bitcast_reduce_fusion), channel_id=2, replica_groups=mesh['seq'=8,'grp'=4] {'grp'}, dimensions={0}, use_global_device_ids=true | all-gather | bytes 2560 | tf_op jit(solution)/shard_map/all_gather | solution.py:24
  117.4 5.3 %all-gather.7.cloned.1.call-done = f32[4,4,2,16,512]{4,3,2,1,0:T(8,128)} async-done(((f32[1,4,2,16,512]{4,3,2,1,0:T(8,128)}), f32[4,4,2,16,512]{4,3,2,1,0:T(8,128)}) %all-gather.7.cloned.1.call-update) | async-done | bytes 1048592 | tf_op jit(solution)/shard_map/all_gather | solution.py:24
  122.7 1.0 slice_bitcast_fusion
  123.7 3.5 %while.19 = (s32[]{:T(128)}, f32[4,2,16]{2,1,0:T(2,128)S(1)}, f32[4,2,16]{2,1,0:T(2,128)S(1)}, f32[4,2,16,512]{3,2,1,0:T(8,128)S(1)}, f32[4,4,2,16]{3,2,1,0:T(2,...) while((s32[]{:T(128)}, f32[4,2,16]{2,1,0:T(2,128)S(1)}, ...), condition=%wide.region_6.7_spmd, body=%wide.region_5.6_spmd.sunk | while | flops 262917 | bytes 792215 | solution.py:29
  123.8 1.1 fusion.54
  124.9 1.1 fusion.54
  126.1 1.1 fusion.54
  127.2 2.0 fusion.24
  129.2 4.2 %fusion.3 = f32[4,2,1792]{2,0,1:T(4,128)S(1)} fusion(bf16[2048,1792]{1,0:T(8,128)(2,1)} %param.15, bf16[16,2,1,4,128]{4,3,2,1,0:T(4,128)(2,1)S(1)} %fusion.24), kind=kOutput, calls=%fused_computation.8 | convolution fusion | flops 58720256 | bytes 7430144 | tf_op jit(solution)/shard_map/dot_general | solution.py:119
  133.5 2.3 %copy.51 = f32[4,2,1792]{0,1,2:T(2,128)} copy(f32[4,2,1792]{2,0,1:T(4,128)S(1)} %fusion.3) | data formatting | bytes 114688
  135.7 3.1 %reshape.78 = f32[1792,8]{1,0:T(8,128)} reshape(f32[1792,2,4]{2,1,0:T(2,128)} %bitcast.134) | data formatting | bytes 114688
  138.9 63.8 %reduce-scatter.4.cloned.1.call-done = f32[224,8]{1,0:T(8,128)} async-done(((f32[1792,8]{1,0:T(8,128)}), f32[224,8]{1,0:T(8,128)}) %reduce-scatter.4.cloned.1.call-update) | async-done | bytes 7184
  202.7 1.0 reshape.79
  203.7 0.1 copy.52
  203.8 0.6 copy.43
  (31 shorter events, 0.5 us)
Async XLA Ops:
  6.5 1.6 copy-start
  6.5 3.6 %copy-start.4 = (s32[4]{0:T(128)S(1)}, s32[4]{0:T(128)}, u32[]{:S(2)}) copy-start(s32[4]{0:T(128)} %param.12) | copy-start | bytes 52
  6.5 48.2 %all-gather.5.cloned.1.call-start = ((), (), s32[]{:S(2)}) async-start(), calls=%async_computation.4 | async-start | bytes 1474560 | tf_op jit(solution)/shard_map/all_gather | solution.py:101
  54.8 2.9 %copy-start.3 = (bf16[4,256,576]{1,2,0:T(8,128)(2,1)S(1)}, bf16[4,256,576]{1,2,0:T(8,128)(2,1)}, u32[]{:S(2)}) copy-start(bf16[4,256,576]{1,2,0:T(8,128)(2,1)} %param.11) | copy-start | bytes 3538948
  58.2 1.0 copy-start.2
  60.1 9.9 %all-to-all-start.1 = ((f32[8,1,128]{2,1,0:T(1,128)}), f32[8,1,128]{2,1,0:T(1,128)S(1)}, u32[]{:S(2)}, u32[]{:S(2)}) async-start(f32[8,1,128]{2,1,0:T(1,128)} %reshape.82), calls=%async_computation.1 | async-start | bytes 8192 | tf_op jit(solution)/shard_map/all_to_all | solution.py:114
  70.0 9.7 %all-to-all-start = ((f32[8,1,128]{2,1,0:T(1,128)}), f32[8,1,128]{2,1,0:T(1,128)S(1)}, u32[]{:S(2)}, u32[]{:S(2)}) async-start(f32[8,1,128]{2,1,0:T(1,128)} %reshape.80), calls=%async_computation | async-start | bytes 8192 | tf_op jit(solution)/shard_map/all_to_all | solution.py:113
  74.3 1.0 copy-start.1
  79.7 26.2 %all-to-all-start.2 = ((bf16[8,1,4,2,16,512]{5,4,3,2,1,0:T(8,128)(2,1)}), bf16[8,1,4,2,16,512]{5,4,3,2,1,0:T(8,128)(2,1)S(1)}, u32[]{:S(2)}, u32[]{:S(2)}) async-start(bf16[8,1,4,2,16,512]{5,4,3,2,1,0:T(8,128)(2,1)} %copy-done.1), calls=%async_computation.2 | async-start | bytes 2097152 | tf_op jit(solution)/shard_map/all_to_all | solution.py:12
  83.3 39.5 %all-gather.7.cloned.1.call-start = ((), (), s32[]{:S(2)}) async-start(), calls=%async_computation.5 | async-start | bytes 1310720 | tf_op jit(solution)/shard_map/all_gather | solution.py:24
  107.0 95.7 %reduce-scatter.4.cloned.1.call-start = ((), (), s32[]{:S(2)}) async-start(), calls=%async_computation.6 | async-start | bytes 1032192
Sparse Core Ops, SparseCore 0:
  10.2 44.5 all-gather.4
  107.1 15.5 all-gather.6
  139.0 63.6 reduce-scatter.3
